TPU v7x, 32 devices: a whole 2x2x4 slice. The times are simulated.
32 devices in a mesh: expert: 4 (over x, core), rows: 8 (over z, y).
Axes of the slice: x: 2, y: 2, z: 4, core: 2. Of those that a mesh axis runs over, the one named last changes fastest.
Arguments:
- step: int32 [], replicated, may hold values from 2 to 8
- gradient: bfloat16 [4, 4096, 14336], P('expert', 'rows'), may hold values from -8 to 8
- weight: bfloat16 [4, 4096, 14336], P('expert', 'rows'), may hold values from -0.119628906 to 0.119628906
- row_state: float32 [4, 4096], P('expert', 'rows'), may hold values from 0.3 to 3
- col_state: float32 [4, 14336], P('expert', 'rows'), may hold values from 0.3 to 3
- prev_msq: float32 [4, 8], P('expert', 'rows'), may hold values from 2 to 500
Outputs:
- new_weight: bfloat16 [4, 4096, 14336], P('expert', 'rows')
- new_row_state: float32 [4, 4096], P('expert', 'rows')
- new_col_state: float32 [4, 14336], P('expert', 'rows')
- new_msq: float32 [4, 8], P('expert', 'rows')
All inputs are finite; a program needn't handle non-finite values.
Results may differ from a plain program's by a relative error of at most 0.001.
Values sent between devices are 32-bit elements; how exact they have to be, the bound alone decides.
A program may use at most 128 MiB of HBM per device.

v0:
```python
import jax
import jax.numpy as jnp
from jax import lax
from jax.sharding import PartitionSpec as P


def shards(step, gradient, weight, row_state, col_state, prev_msq):
    local_experts = gradient.shape[0]
    local_rows = gradient.shape[1]
    columns = gradient.shape[2]
    row_devices = lax.axis_size("rows")
    expert_devices = lax.axis_size("expert")
    all_rows = local_rows * row_devices
    beta = 1.0 - step.astype(jnp.float32) ** (-0.8)
    grad = gradient.astype(jnp.float32)
    squares = grad * grad + 1e-30
    new_row = beta * row_state + (1.0 - beta) * jnp.mean(squares, axis=2)
    partial_cols = jnp.sum(squares, axis=1)
    clip_term = jnp.sum(prev_msq)
    row_sum = jnp.sum(new_row, axis=1)
    clip_total = lax.psum(clip_term, ("expert", "rows"))
    row_totals = lax.psum(row_sum, "rows")
    entries = prev_msq.shape[0] * prev_msq.shape[1] * expert_devices * row_devices
    clip = jnp.sqrt(clip_total / entries)
    row_mean = row_totals / all_rows
    old_full = lax.all_gather(col_state, "rows", axis=1, tiled=True)
    col_totals = lax.psum(partial_cols, "rows")
    full_cols = beta * old_full + (1.0 - beta) * col_totals / all_rows
    width = columns // row_devices
    new_col = lax.dynamic_slice_in_dim(full_cols, lax.axis_index("rows") * width, width, 1)
    scaled = new_row[:, :, None] * full_cols[:, None, :] / row_mean[:, None, None]
    update = grad / jnp.sqrt(scaled) / clip
    new_weight = (weight.astype(jnp.float32) - 0.01 * update).astype(jnp.bfloat16)
    new_msq = jnp.mean(update * update, axis=(1, 2)).reshape(local_experts, 1)
    return (new_weight, new_row, new_col, new_msq)


def solution(mesh):
    placed = (
        P(),
        P("expert", "rows", None),
        P("expert", "rows", None),
        P("expert", "rows"),
        P("expert", "rows"),
        P("expert", "rows"),
    )
    return jax.shard_map(
        shards,
        mesh=mesh,
        in_specs=placed,
        out_specs=(
            P("expert", "rows", None),
            P("expert", "rows"),
            P("expert", "rows"),
            P("expert", "rows"),
        ),
        check_vma=False,
    )
```

profile of v0, /device:TPU:0, one launch (start us, length us, event | category | flops | bytes accessed | tf_op | source)
XLA Modules:
  0.0 154.7 jit_solution(15498681350571910622)
XLA Ops:
  0.6 0.0 copy-start.2
  0.6 0.0 copy-start.1
  1.4 20.0 %fusion.1 = (f32[14336]{0:T(1024)S(1)}, f32[512]{0:T(512)S(1)}) fusion(bf16[1,512,14336]{2,1,0:T(8,128)(2,1)} %param.7), kind=kLoop, calls=%fused_computation.3 | loop fusion | flops 36685312 | bytes 14739456 | tf_op jit(solution)/shard_map/reduce_sum | solution.py:18
  21.4 0.0 copy-done.2
  21.4 0.6 fusion.4
  22.0 0.0 copy-start
  22.0 39.4 %all-reduce = (f32[1]{0:T(128)}, f32[1,14336]{1,0:T(1,128)S(1)}) all-reduce(f32[1]{0:T(128)} %bitcast.4, f32[1,14336]{1,0:T(1,128)S(1)} %bitcast.9), channel_id=1, replica_groups=mesh['expert'=4,'rows'=8] {'rows'}, use_global_device_ids=true, to_apply=%region_4.0 | all-reduce | flops 14337 | bytes 114696 | tf_op jit(solution)/shard_map/psum | solution.py:22
  61.4 0.0 copy-done.1
  61.4 30.7 %all_gather.3 = f32[1,14336]{1,0:T(1,128)S(1)} all-gather(f32[1,1792]{1,0:T(1,128)S(1)} %copy-done.1), channel_id=1, replica_groups=mesh['expert'=4,'rows'=8] {'rows'}, dimensions={1}, use_global_device_ids=true | all-gather | bytes 64512 | tf_op jit(solution)/shard_map/all_gather | solution.py:26
  92.1 0.1 multiply_add_fusion
  92.9 37.1 %psum.23 = f32[]{:T(128)} all-reduce(f32[]{:T(128)} %bitcast.6), channel_id=1, replica_groups=mesh['expert'=4,'rows'=8] {'expert','rows'}, use_global_device_ids=true, to_apply=%region_5.0 | all-reduce | flops 1 | bytes 8 | tf_op jit(solution)/shard_map/psum | solution.py:21
  130.6 21.7 %multiply_reduce_fusion = (f32[]{:T(128)}, bf16[1,512,14336]{2,1,0:T(8,128)(2,1)}) fusion(f32[]{:T(128)S(6)} %sqrt.7, f32[]{:T(128)} %bitcast.5, f32[14336]{0:T(1024)S(1)} %bitcast.8, f32[512]{0:T(512)S(1)} %bitcast.10, bf16[1,512,14336]{2,1,0:T(8,128)(2,1)} %param.7, bf16[1,512,14336]{2,1,0:T(8,128)(2,1)} %param.8), kind=kLoop, calls=%fused_computation.6 | loop fusion | flops 80740352 | bytes 44099596 | tf_op jit(solution)/shard_map/reduce_sum | solution.py:34
  152.3 0.0 copy-done
  153.0 0.6 constant_dynamic-slice_fusion
  (1 shorter events, 0.0 us)
Async XLA Ops:
  0.6 20.8 %copy-start.2 = (f32[1,512]{1,0:T(1,128)S(1)}, f32[1,512]{1,0:T(1,128)}, u32[]{:S(2)}) copy-start(f32[1,512]{1,0:T(1,128)} %param.9) | copy-start | bytes 6148
  0.6 60.8 %copy-start.1 = (f32[1,1792]{1,0:T(1,128)S(1)}, f32[1,1792]{1,0:T(1,128)}, u32[]{:S(2)}) copy-start(f32[1,1792]{1,0:T(1,128)} %param.10) | copy-start | bytes 21508
  22.0 130.3 %copy-start = (f32[1,512]{1,0:T(1,128)}, f32[1,512]{1,0:T(1,128)S(1)}, u32[]{:S(2)}) copy-start(f32[1,512]{1,0:T(1,128)S(1)} %get-tuple-element.9) | copy-start | bytes 6148
where the time goes:
time: 156 us; the launch traced here: 155 us
  blocking collectives  107 us (69%)
  other arithmetic  42.4 us (27%)
  between operations  4.54 us (3%)
    psum x1, blocking collectives, shards(): row_totals = lax.psum(row_sum, 'rows')  39.4 us
    psum x1, blocking collectives, shards(): clip_total = lax.psum(clip_term, ('expert', 'rows'))  37.1 us
    all_gather x1, blocking collectives, shards(): old_full = lax.all_gather(col_state, 'rows', axis=1, tiled=True)  30.7 us
    reduce_sum x1, other arithmetic, shards(): new_msq = jnp.mean(update * update, axis=(1, 2)).reshape(local_experts, 1)  21.7 us
    reduce_sum x1, other arithmetic, shards(): partial_cols = jnp.sum(squares, axis=1)  20 us

commit v1 on v0

v1 whole, which is shorter than its diff:
```python
import functools

import jax
import jax.numpy as jnp
from jax import lax
from jax.experimental import pallas as pl
from jax.experimental.pallas import tpu as pltpu
from jax.sharding import PartitionSpec as P

MESH = pl.DeviceIdType.MESH
RATE = 0.01
TINY = 1e-30
LANES = 128
ROWS = 16


def lane_sum(x):
    total = x[:, :LANES]
    for k in range(1, x.shape[1] // LANES):
        total = total + x[:, k * LANES : (k + 1) * LANES]
    return total


def statistics_kernel(
    n, experts, step_ref, prev_ref, row_ref, col_ref, g_hbm, w_hbm,
    g_out, w_out, scale_out, factor_out, new_row_out, new_col_out,
    acc, part, parts_in, message, messages_in, clip_out, clips_in,
    g_sem, w_sem, clip_send, clip_recv, part_send, part_recv, gather_send, gather_recv,
):
    me = lax.axis_index("rows")
    mine = lax.axis_index("expert")
    rows, columns = g_out.shape
    width = columns // n

    def column_slice(c):
        return pl.ds(pl.multiple_of(c * width, LANES), width)

    def chunk_of(s):
        return lax.rem(me + (2 * (s % 2) - 1) * ((n - s) // 2) + n, n)

    def g_copy(s):
        cols = column_slice(chunk_of(s))
        return pltpu.make_async_copy(g_hbm.at[:, cols], g_out.at[:, cols], g_sem.at[s])

    def w_copy(s):
        cols = column_slice(s)
        return pltpu.make_async_copy(w_hbm.at[:, cols], w_out.at[:, cols], w_sem.at[s])

    def clip_copy(k):
        peer = lax.rem(mine + k, experts)
        return pltpu.make_async_remote_copy(
            src_ref=clip_out, dst_ref=clips_in.at[k - 1], send_sem=clip_send.at[k - 1],
            recv_sem=clip_recv.at[k - 1], device_id={"expert": peer}, device_id_type=MESH,
        )

    def part_copy(s):
        c = chunk_of(s)
        return pltpu.make_async_remote_copy(
            src_ref=part.at[s], dst_ref=parts_in.at[s], send_sem=part_send.at[s],
            recv_sem=part_recv.at[s], device_id={"rows": c}, device_id_type=MESH,
        )

    def gather_copy(k):
        peer = lax.rem(me + k, n)
        return pltpu.make_async_remote_copy(
            src_ref=message, dst_ref=messages_in.at[k - 1], send_sem=gather_send.at[k - 1],
            recv_sem=gather_recv.at[k - 1], device_id={"rows": peer}, device_id_type=MESH,
        )

    for s in range(n):
        g_copy(s).start()

    barrier = pltpu.get_barrier_semaphore()
    for k in range(1, n):
        pl.semaphore_signal(barrier, inc=1, device_id={"rows": lax.rem(me + k, n)}, device_id_type=MESH)
    for k in range(1, experts):
        pl.semaphore_signal(barrier, inc=1, device_id={"expert": lax.rem(mine + k, experts)}, device_id_type=MESH)

    acc[...] = jnp.zeros_like(acc)
    clip_out[...] = jnp.full((1, LANES), prev_ref[0], jnp.float32)
    beta = 1.0 - jnp.exp(-0.8 * jnp.log(jnp.full((1, LANES), step_ref[0], jnp.int32).astype(jnp.float32)))

    def chunk(s):
        cols = column_slice(chunk_of(s))
        g_copy(s).wait()

        def body(i, carry):
            at = pl.ds(pl.multiple_of(i * ROWS, ROWS), ROWS)
            x = g_out[at, cols].astype(jnp.float32)
            squares = x * x
            acc[at, :] += lane_sum(squares)
            return carry + (squares[: ROWS // 2] + squares[ROWS // 2 :])

        col = lax.fori_loop(0, rows // ROWS, body, jnp.zeros((ROWS // 2, width), jnp.float32))
        part[s] = jnp.sum(col, axis=0, keepdims=True)

    half = n // 2

    @pl.loop(0, half)
    def _(s):
        chunk(s)

    pl.semaphore_wait(barrier, n - 1 + experts - 1)
    for k in range(1, experts):
        clip_copy(k).start()
    for s in range(half):
        part_copy(s).start()

    @pl.loop(half, n - 1)
    def _(s):
        w_copy(s - half).start()
        chunk(s)
        part_copy(s).start()

    for s in range(n - 1 - half, n):
        w_copy(s).start()
    chunk(n - 1)

    share = lane_sum(row_ref[...]) * beta
    share = share + (1.0 - beta) * (jnp.sum(acc[...], axis=0, keepdims=True) * (1.0 / columns) + TINY * (rows / LANES))
    clips = clip_out[...]
    for k in range(1, experts):
        clip_copy(k).wait()
        clips = clips + clips_in[k - 1]
    total = part[n - 1]
    for s in range(n - 1):
        part_copy(s).wait()
        total = total + parts_in[s]
    beta_cols = jnp.concatenate([beta] * (width // LANES), axis=1)
    new_col = beta_cols * col_ref[...] + (1.0 - beta_cols) * (total * (1.0 / (rows * n)) + TINY)
    message[:, :width] = new_col
    message[:, width : width + LANES] = share
    message[:, width + LANES :] = clips
    for k in range(1, n):
        gather_copy(k).start()

    new_col_out[...] = new_col
    factor_out[:, column_slice(me)] = lax.rsqrt(new_col)
    sums = jnp.sum(jnp.transpose(acc[...]), axis=0, keepdims=True)
    beta_rows = jnp.concatenate([beta] * (rows // LANES), axis=1)
    new_row = beta_rows * row_ref[...] + (1.0 - beta_rows) * (sums * (1.0 / columns) + TINY)
    new_row_out[...] = new_row
    for s in range(n):
        w_copy(s).wait()

    for k in range(1, n):
        gather_copy(k).wait()
        source = lax.rem(me - k + n, n)
        factor_out[:, column_slice(source)] = lax.rsqrt(messages_in[k - 1, :, :width])
        share = share + messages_in[k - 1, :, width : width + LANES]
        clips = clips + messages_in[k - 1, :, width + LANES :]
    row_mean = jnp.sum(share, axis=1, keepdims=True) * (1.0 / (rows * n))
    clip = jnp.sqrt(clips[:, :1] * (1.0 / (n * experts)))
    scale = lax.rsqrt(new_row / row_mean) * (RATE / clip)
    scale_out[...] = jnp.transpose(jnp.broadcast_to(scale, (LANES, rows)))


def update_kernel(
    block, g_ref, w_ref, scale_ref, factor_ref, row_ref, col_ref,
    new_w_hbm, new_row_out, new_col_out, msq_out, stage, sem,
):
    rows, columns = g_ref.shape
    blocks = columns // block

    def out_copy(b):
        cols = pl.ds(pl.multiple_of(b * block, LANES), block)
        return pltpu.make_async_copy(stage.at[b % 2], new_w_hbm.at[:, cols], sem.at[b % 2])

    new_row_out[...] = row_ref[...]
    new_col_out[...] = col_ref[...]

    def do_block(b, total):
        cols = pl.ds(pl.multiple_of(b * block, LANES), block)
        slot = b % 2

        @pl.when(b >= 2)
        def _():
            out_copy(b - 2).wait()

        factor = jnp.broadcast_to(factor_ref[:, cols], (ROWS, block))

        def body(i, total):
            at = pl.ds(pl.multiple_of(i * ROWS, ROWS), ROWS)
            scale = jnp.concatenate([scale_ref[at, :]] * (block // LANES), axis=1)
            move = g_ref[at, cols].astype(jnp.float32) * factor * scale
            stage[slot, at, :] = (w_ref[at, cols].astype(jnp.float32) - move).astype(jnp.bfloat16)
            return total + lane_sum(move * move)

        total = lax.fori_loop(0, rows // ROWS, body, total)
        out_copy(b).start()
        return total

    total = lax.fori_loop(0, blocks, do_block, jnp.zeros((ROWS, LANES), jnp.float32))
    for b in range(max(blocks - 2, 0), blocks):
        out_copy(b).wait()
    msq = jnp.sum(jnp.sum(total, axis=0, keepdims=True), axis=1, keepdims=True)
    msq_out[...] = msq * (1.0 / (RATE * RATE * rows * columns))


def block_width(columns):
    tiles = columns // LANES
    for d in (8, 7, 4, 2, 1):
        if tiles % d == 0:
            return d * LANES


def shards(step, gradient, weight, row_state, col_state, prev_msq):
    _, rows, columns = gradient.shape
    n = lax.axis_size("rows")
    experts = lax.axis_size("expert")
    width = columns // n
    f32, bf16 = jnp.float32, gradient.dtype
    vmem = pl.BlockSpec(memory_space=pltpu.VMEM)
    smem = pl.BlockSpec(memory_space=pltpu.SMEM)
    anywhere = pl.BlockSpec(memory_space=pl.ANY)
    dma = pltpu.SemaphoreType.DMA
    big = rows * columns * 2
    g, w, scale, factor, new_row, new_col = pl.pallas_call(
        functools.partial(statistics_kernel, n, experts),
        out_shape=[
            pltpu.VMEM((rows, columns), bf16),
            pltpu.VMEM((rows, columns), bf16),
            pltpu.VMEM((rows, LANES), f32),
            pltpu.VMEM((1, columns), f32),
            pltpu.VMEM((1, rows), f32),
            pltpu.VMEM((1, width), f32),
        ],
        in_specs=[smem, smem, vmem, vmem, anywhere, anywhere],
        out_specs=[vmem] * 6,
        scratch_shapes=[
            pltpu.VMEM((rows, LANES), f32),
            pltpu.VMEM((n, 1, width), f32),
            pltpu.VMEM((n - 1, 1, width), f32),
            pltpu.VMEM((1, width + 2 * LANES), f32),
            pltpu.VMEM((n - 1, 1, width + 2 * LANES), f32),
            pltpu.VMEM((1, LANES), f32),
            pltpu.VMEM((experts - 1, 1, LANES), f32),
            dma((n,)), dma((n,)), dma((experts - 1,)), dma((experts - 1,)),
            dma((n - 1,)), dma((n - 1,)), dma((n - 1,)), dma((n - 1,)),
        ],
        compiler_params=pltpu.CompilerParams(
            collective_id=0, has_side_effects=True, vmem_limit_bytes=8 * 2**20
        ),
        name="statistics",
    )(
        step.reshape(1), prev_msq.reshape(1), row_state, col_state,
        gradient.reshape(rows, columns), weight.reshape(rows, columns),
    )
    block = block_width(columns)
    g, w, scale, factor, new_row, new_col = (
        pltpu.with_memory_space_constraint(x, pltpu.VMEM) for x in (g, w, scale, factor, new_row, new_col)
    )
    new_weight, new_row, new_col, msq = pl.pallas_call(
        functools.partial(update_kernel, block),
        out_shape=[
            jax.ShapeDtypeStruct((rows, columns), bf16),
            jax.ShapeDtypeStruct((1, rows), f32),
            jax.ShapeDtypeStruct((1, width), f32),
            jax.ShapeDtypeStruct((1, 1), f32),
        ],
        in_specs=[vmem] * 6,
        out_specs=[anywhere, vmem, vmem, vmem],
        scratch_shapes=[pltpu.VMEM((2, rows, block), bf16), dma((2,))],
        compiler_params=pltpu.CompilerParams(vmem_limit_bytes=8 * 2**20),
        name="update",
    )(g, w, scale, factor, new_row, new_col)
    return (new_weight.reshape(1, rows, columns), new_row, new_col, msq)


def solution(mesh):
    split = P("expert", "rows")
    whole = P("expert", "rows", None)
    return jax.shard_map(
        shards,
        mesh=mesh,
        in_specs=(P(), whole, whole, split, split, split),
        out_specs=(whole, split, split, split),
        check_vma=False,
    )
```

time: 156 us -> 64.6 us (0.41)
  blocking collectives: 107 us -> 0 us
  other arithmetic: 42.4 us -> 0 us
  Pallas kernels: 0 us -> 34.8 us
  local copies, waits for them, and re-layouts: 0.61 us -> 27.5 us
  between operations: 4.54 us -> 1.95 us
    psum x2 -> x0, blocking collectives: 76.5 us -> none  [the longest x1 39.4 us: shards(): row_totals = lax.psum(row_sum, 'rows')]
    reduce_sum x3 -> x0, other arithmetic: 42.3 us -> none  [the longest x1 21.7 us: shards(): new_msq = jnp.mean(update * update, axis=(1, 2)).reshape(local_experts, 1)]
    pallas_call x0 -> x2, Pallas kernels: none -> 34.8 us  [the longest x1 21.2 us: shards(): pl.pallas_call(functools.partial(statistics_kernel, n, experts), out_shap...]
    all_gather x1 -> x0, blocking collectives: 30.7 us -> none  [shards(): old_full = lax.all_gather(col_state, 'rows', axis=1, tiled=True)]
    unnamed x6 -> x14, local copies, waits for them, and re-layouts: 0.01 us -> 27.5 us
where the time goes in v1:
time: 64.6 us; the launch traced here: 64.3 us
  Pallas kernels  34.8 us (54%)
  local copies, waits for them, and re-layouts  27.5 us (43%)
  between operations  1.95 us (3%)
    unnamed x14, local copies, waits for them, and re-layouts  27.5 us
    pallas_call x1, Pallas kernels, shards(): pl.pallas_call(functools.partial(statistics_kernel, n, experts), out_shap...  21.2 us
    pallas_call x1, Pallas kernels, shards(): pl.pallas_call(functools.partial(update_kernel, block), out_shape=[jax.Sh...  13.6 us

profile of v1, /device:TPU:0, one launch (start us, length us, event | category | flops | bytes accessed | tf_op | source)
XLA Modules:
  0.0 64.3 jit_solution(9975429177238659416)
XLA Ops:
  1.9 0.0 copy-start.4
  1.9 5.2 %copy-done.4 = bf16[1,512,14336]{2,1,0:T(8,128)(2,1)S(1)} copy-done((bf16[1,512,14336]{2,1,0:T(8,128)(2,1)S(1)}, bf16[1,512,14336]{2,1,0:T(8,128)(2,1)}, u32[]{:S(2)}) %copy-start.4) | copy-done | bytes 14680088
  7.1 0.0 copy-start.5
  7.1 0.7 %copy-done.5 = f32[1,1792]{1,0:T(1,128)S(1)} copy-done((f32[1,1792]{1,0:T(1,128)S(1)}, f32[1,1792]{1,0:T(1,128)}, u32[]{:S(2)}) %copy-start.5) | copy-done | bytes 7192
  7.8 0.0 copy-start.6
  7.8 0.7 %copy-done.6 = f32[1,512]{1,0:T(1,128)S(1)} copy-done((f32[1,512]{1,0:T(1,128)S(1)}, f32[1,512]{1,0:T(1,128)}, u32[]{:S(2)}) %copy-start.6) | copy-done | bytes 2072
  8.5 21.2 %statistics.1 = (bf16[512,14336]{1,0:T(8,128)(2,1)S(1)}, bf16[512,14336]{1,0:T(8,128)(2,1)S(1)}, f32[512,128]{1,0:T(8,128)S(1)}, f32[1,14336]{1,0:T(1,128)S(1)},...) custom-call(s32[1]{0:T(128)} %bitcast.5.step_ref, f32[1]{0:T(128)} %bitcast.6.prev_ref, f32[1,512]{1,0:T(1,128)S(1)} %copy-done.6, ...), custom_call_target="tpu_custom_call" | custom-call | tf_op jit(solution)/shard_map/statistics/pallas_call | solution.py:218
  29.7 0.0 copy-start
  29.7 5.5 %copy-done = bf16[512,14336]{1,0:T(8,128)(2,1)} copy-done((bf16[512,14336]{1,0:T(8,128)(2,1)}, bf16[512,14336]{1,0:T(8,128)(2,1)S(1)}, u32[]{:S(2)}) %copy-start) | copy-done | bytes 14680088
  35.2 0.0 copy-start.2
  35.2 5.2 %copy-done.2 = bf16[512,14336]{1,0:T(8,128)(2,1)} copy-done((bf16[512,14336]{1,0:T(8,128)(2,1)}, bf16[512,14336]{1,0:T(8,128)(2,1)S(1)}, u32[]{:S(2)}) %copy-start.2) | copy-done | bytes 14680088
  40.4 0.0 copy-start.1
  40.4 5.2 %copy-done.1 = bf16[512,14336]{1,0:T(8,128)(2,1)S(1)} copy-done((bf16[512,14336]{1,0:T(8,128)(2,1)S(1)}, bf16[512,14336]{1,0:T(8,128)(2,1)}, u32[]{:S(2)}) %copy-start.1) | copy-done | bytes 14680088
  45.6 0.0 copy-start.3
  45.6 5.2 %copy-done.3 = bf16[512,14336]{1,0:T(8,128)(2,1)S(1)} copy-done((bf16[512,14336]{1,0:T(8,128)(2,1)S(1)}, bf16[512,14336]{1,0:T(8,128)(2,1)}, u32[]{:S(2)}) %copy-start.3) | copy-done | bytes 14680088
  50.7 13.6 %update.1 = (bf16[512,14336]{1,0:T(8,128)(2,1)}, f32[1,512]{1,0:T(1,128)}, f32[1,1792]{1,0:T(1,128)}, f32[1,1]{1,0:T(1,128)}) custom-call(bf16[512,14336]{1,0:T(8,128)(2,1)S(1)} %copy-done.1, bf16[512,14336]{1,0:T(8,128)(2,1)S(1)} %copy-done.3, f32[512,128]{1,0:T(8,128)S(1)} %get-tuple-element.16.scale_ref, f32[1,14336]{1,0:T(1,128)S(1)} %get-tuple-element.17.factor_ref, ...), custom_call_target="tpu_custom_call" | custom-call | tf_op jit(solution)/shard_map/update/pallas_call | solution.py:253
Async XLA Ops:
  1.9 5.2 %copy-start.4 = (bf16[1,512,14336]{2,1,0:T(8,128)(2,1)S(1)}, bf16[1,512,14336]{2,1,0:T(8,128)(2,1)}, u32[]{:S(2)}) copy-start(bf16[1,512,14336]{2,1,0:T(8,128)(2,1)} %param.7) | copy-start | bytes 44040196
  7.1 0.7 %copy-start.5 = (f32[1,1792]{1,0:T(1,128)S(1)}, f32[1,1792]{1,0:T(1,128)}, u32[]{:S(2)}) copy-start(f32[1,1792]{1,0:T(1,128)} %col_ref.1) | copy-start | bytes 21508
  7.8 0.7 %copy-start.6 = (f32[1,512]{1,0:T(1,128)S(1)}, f32[1,512]{1,0:T(1,128)}, u32[]{:S(2)}) copy-start(f32[1,512]{1,0:T(1,128)} %row_ref.1) | copy-start | bytes 6148
  29.7 5.5 %copy-start = (bf16[512,14336]{1,0:T(8,128)(2,1)}, bf16[512,14336]{1,0:T(8,128)(2,1)S(1)}, u32[]{:S(2)}) copy-start(bf16[512,14336]{1,0:T(8,128)(2,1)S(1)} %get-tuple-element.14.g_ref) | copy-start | bytes 44040196
  35.2 5.2 %copy-start.2 = (bf16[512,14336]{1,0:T(8,128)(2,1)}, bf16[512,14336]{1,0:T(8,128)(2,1)S(1)}, u32[]{:S(2)}) copy-start(bf16[512,14336]{1,0:T(8,128)(2,1)S(1)} %get-tuple-element.15.w_ref) | copy-start | bytes 44040196
  40.4 5.2 %copy-start.1 = (bf16[512,14336]{1,0:T(8,128)(2,1)S(1)}, bf16[512,14336]{1,0:T(8,128)(2,1)}, u32[]{:S(2)}) copy-start(bf16[512,14336]{1,0:T(8,128)(2,1)} %copy-done) | copy-start | bytes 44040196
  45.6 5.2 %copy-start.3 = (bf16[512,14336]{1,0:T(8,128)(2,1)S(1)}, bf16[512,14336]{1,0:T(8,128)(2,1)}, u32[]{:S(2)}) copy-start(bf16[512,14336]{1,0:T(8,128)(2,1)} %copy-done.2) | copy-start | bytes 44040196

commit v2 on v1

--- a/solution.py
+++ b/solution.py
@@ -22,10 +22,10 @@
 
 
 def statistics_kernel(
-    n, experts, step_ref, prev_ref, row_ref, col_ref, g_hbm, w_hbm,
+    n, experts, step_ref, prev_ref, row_hbm, col_hbm, g_hbm, w_hbm,
     g_out, w_out, scale_out, factor_out, new_row_out, new_col_out,
     acc, part, parts_in, message, messages_in, clip_out, clips_in,
-    g_sem, w_sem, clip_send, clip_recv, part_send, part_recv, gather_send, gather_recv,
+    row_ref, col_ref, small_sem, g_sem, w_sem, clip_send, clip_recv, part_send, part_recv, gather_send, gather_recv,
 ):
     me = lax.axis_index("rows")
     mine = lax.axis_index("expert")
@@ -67,6 +67,10 @@
             recv_sem=gather_recv.at[k - 1], device_id={"rows": peer}, device_id_type=MESH,
         )
 
+    pairs = ((row_hbm, row_ref), (col_hbm, col_ref))
+    small = [pltpu.make_async_copy(src, dst, small_sem.at[k]) for k, (src, dst) in enumerate(pairs)]
+    for copy in small:
+        copy.start()
     for s in range(n):
         g_copy(s).start()
 
@@ -77,6 +81,8 @@
         pl.semaphore_signal(barrier, inc=1, device_id={"expert": lax.rem(mine + k, experts)}, device_id_type=MESH)
 
     acc[...] = jnp.zeros_like(acc)
+    for copy in small:
+        copy.wait()
     clip_out[...] = jnp.full((1, LANES), prev_ref[0], jnp.float32)
     beta = 1.0 - jnp.exp(-0.8 * jnp.log(jnp.full((1, LANES), step_ref[0], jnp.int32).astype(jnp.float32)))
 
@@ -211,8 +217,7 @@
     width = columns // n
     f32, bf16 = jnp.float32, gradient.dtype
     vmem = pl.BlockSpec(memory_space=pltpu.VMEM)
-    smem = pl.BlockSpec(memory_space=pltpu.SMEM)
-    anywhere = pl.BlockSpec(memory_space=pl.ANY)
+    hbm = pl.BlockSpec(memory_space=pltpu.HBM)
     dma = pltpu.SemaphoreType.DMA
     big = rows * columns * 2
     g, w, scale, factor, new_row, new_col = pl.pallas_call(
@@ -225,7 +230,7 @@
             pltpu.VMEM((1, rows), f32),
             pltpu.VMEM((1, width), f32),
         ],
-        in_specs=[smem, smem, vmem, vmem, anywhere, anywhere],
+        in_specs=[pl.BlockSpec(memory_space=pltpu.SMEM)] * 2 + [hbm] * 4,
         out_specs=[vmem] * 6,
         scratch_shapes=[
             pltpu.VMEM((rows, LANES), f32),
@@ -235,7 +240,9 @@
             pltpu.VMEM((n - 1, 1, width + 2 * LANES), f32),
             pltpu.VMEM((1, LANES), f32),
             pltpu.VMEM((experts - 1, 1, LANES), f32),
-            dma((n,)), dma((n,)), dma((experts - 1,)), dma((experts - 1,)),
+            pltpu.VMEM((1, rows), f32),
+            pltpu.VMEM((1, width), f32),
+            dma((2,)), dma((n,)), dma((n,)), dma((experts - 1,)), dma((experts - 1,)),
             dma((n - 1,)), dma((n - 1,)), dma((n - 1,)), dma((n - 1,)),
         ],
         compiler_params=pltpu.CompilerParams(
@@ -243,13 +250,13 @@
         ),
         name="statistics",
     )(
-        step.reshape(1), prev_msq.reshape(1), row_state, col_state,
-        gradient.reshape(rows, columns), weight.reshape(rows, columns),
+        step.reshape(1), prev_msq.reshape(1),
+        *(
+            pltpu.with_memory_space_constraint(x, pltpu.HBM)
+            for x in (row_state, col_state, gradient.reshape(rows, columns), weight.reshape(rows, columns))
+        )
     )
     block = block_width(columns)
-    g, w, scale, factor, new_row, new_col = (
-        pltpu.with_memory_space_constraint(x, pltpu.VMEM) for x in (g, w, scale, factor, new_row, new_col)
-    )
     new_weight, new_row, new_col, msq = pl.pallas_call(
         functools.partial(update_kernel, block),
         out_shape=[
@@ -259,7 +266,7 @@
             jax.ShapeDtypeStruct((1, 1), f32),
         ],
         in_specs=[vmem] * 6,
-        out_specs=[anywhere, vmem, vmem, vmem],
+        out_specs=[hbm, vmem, vmem, vmem],
         scratch_shapes=[pltpu.VMEM((2, rows, block), bf16), dma((2,))],
         compiler_params=pltpu.CompilerParams(vmem_limit_bytes=8 * 2**20),
         name="update",

time: 64.6 us -> 37.5 us (0.58)
  local copies, waits for them, and re-layouts: 27.5 us -> 0 us
    unnamed x14 -> x0, local copies, waits for them, and re-layouts: 27.5 us -> none
where the time goes in v2:
time: 37.5 us; the launch traced here: 37.3 us
  Pallas kernels  35.4 us (94%)
  between operations  1.93 us (5%)
    pallas_call x1, Pallas kernels, shards(): pl.pallas_call(functools.partial(statistics_kernel, n, experts), out_shap...  21.8 us
    pallas_call x1, Pallas kernels, shards(): pl.pallas_call(functools.partial(update_kernel, block), out_shape=[jax.Sh...  13.6 us

profile of v2, /device:TPU:0, one launch (start us, length us, event | category | flops | bytes accessed | tf_op | source)
XLA Modules:
  0.0 37.3 jit_solution(11944538618337892550)
XLA Ops:
  1.9 21.8 %statistics.1 = (bf16[512,14336]{1,0:T(8,128)(2,1)S(1)}, bf16[512,14336]{1,0:T(8,128)(2,1)S(1)}, f32[512,128]{1,0:T(8,128)S(1)}, f32[1,14336]{1,0:T(1,128)S(1)},...) custom-call(s32[1]{0:T(128)} %bitcast.5.step_ref, f32[1]{0:T(128)} %bitcast.6.prev_ref, f32[1,512]{1,0:T(1,128)} %row_hbm.1, ...), custom_call_target="tpu_custom_call" | custom-call | tf_op jit(solution)/shard_map/statistics/pallas_call | solution.py:223
  23.8 13.6 %update.1 = (bf16[512,14336]{1,0:T(8,128)(2,1)}, f32[1,512]{1,0:T(1,128)}, f32[1,1792]{1,0:T(1,128)}, f32[1,1]{1,0:T(1,128)}) custom-call(bf16[512,14336]{1,0:T(8,128)(2,1)S(1)} %get-tuple-element.14.g_ref, bf16[512,14336]{1,0:T(8,128)(2,1)S(1)} %get-tuple-element.15.w_ref, f32[512,128]{1,0:T(8,128)S(1)} %get-tuple-element.16.scale_ref, ...), custom_call_target="tpu_custom_call" | custom-call | tf_op jit(solution)/shard_map/update/pallas_call | solution.py:260

commit v3 on v2

--- a/solution.py
+++ b/solution.py
@@ -12,6 +12,7 @@
 TINY = 1e-30
 LANES = 128
 ROWS = 16
+UNROLL = 4
 
 
 def lane_sum(x):
@@ -35,8 +36,15 @@
     def column_slice(c):
         return pl.ds(pl.multiple_of(c * width, LANES), width)
 
+    def partner(k):
+        peer, bit = 0, 1
+        while bit < n:
+            peer = peer + bit * ((me // bit + k // bit) % 2)
+            bit *= 2
+        return peer
+
     def chunk_of(s):
-        return lax.rem(me + (2 * (s % 2) - 1) * ((n - s) // 2) + n, n)
+        return partner(n - 1 - s)
 
     def g_copy(s):
         cols = column_slice(chunk_of(s))
@@ -61,7 +69,7 @@
         )
 
     def gather_copy(k):
-        peer = lax.rem(me + k, n)
+        peer = partner(k)
         return pltpu.make_async_remote_copy(
             src_ref=message, dst_ref=messages_in.at[k - 1], send_sem=gather_send.at[k - 1],
             recv_sem=gather_recv.at[k - 1], device_id={"rows": peer}, device_id_type=MESH,
@@ -97,7 +105,7 @@
             acc[at, :] += lane_sum(squares)
             return carry + (squares[: ROWS // 2] + squares[ROWS // 2 :])
 
-        col = lax.fori_loop(0, rows // ROWS, body, jnp.zeros((ROWS // 2, width), jnp.float32))
+        col = lax.fori_loop(0, rows // ROWS, body, jnp.zeros((ROWS // 2, width), jnp.float32), unroll=UNROLL)
         part[s] = jnp.sum(col, axis=0, keepdims=True)
 
     half = n // 2
@@ -114,12 +122,12 @@
 
     @pl.loop(half, n - 1)
     def _(s):
-        w_copy(s - half).start()
+        w_copy(s - half).start(priority=1)
         chunk(s)
         part_copy(s).start()
 
     for s in range(n - 1 - half, n):
-        w_copy(s).start()
+        w_copy(s).start(priority=1)
     chunk(n - 1)
 
     share = lane_sum(row_ref[...]) * beta
@@ -137,28 +145,28 @@
     message[:, :width] = new_col
     message[:, width : width + LANES] = share
     message[:, width + LANES :] = clips
-    for k in range(1, n):
+    for k in reversed(range(1, n)):
         gather_copy(k).start()
 
     new_col_out[...] = new_col
-    factor_out[:, column_slice(me)] = lax.rsqrt(new_col)
     sums = jnp.sum(jnp.transpose(acc[...]), axis=0, keepdims=True)
     beta_rows = jnp.concatenate([beta] * (rows // LANES), axis=1)
     new_row = beta_rows * row_ref[...] + (1.0 - beta_rows) * (sums * (1.0 / columns) + TINY)
     new_row_out[...] = new_row
+    scale_out[...] = jnp.transpose(jnp.broadcast_to(lax.rsqrt(new_row), (LANES, rows)))
     for s in range(n):
         w_copy(s).wait()
 
-    for k in range(1, n):
+    for k in reversed(range(1, n)):
         gather_copy(k).wait()
-        source = lax.rem(me - k + n, n)
-        factor_out[:, column_slice(source)] = lax.rsqrt(messages_in[k - 1, :, :width])
         share = share + messages_in[k - 1, :, width : width + LANES]
         clips = clips + messages_in[k - 1, :, width + LANES :]
     row_mean = jnp.sum(share, axis=1, keepdims=True) * (1.0 / (rows * n))
-    clip = jnp.sqrt(clips[:, :1] * (1.0 / (n * experts)))
-    scale = lax.rsqrt(new_row / row_mean) * (RATE / clip)
-    scale_out[...] = jnp.transpose(jnp.broadcast_to(scale, (LANES, rows)))
+    clip_square = clips[:, :1] * (1.0 / (n * experts))
+    common = RATE * jnp.sqrt(row_mean) * lax.rsqrt(clip_square)
+    factor_out[:, column_slice(me)] = lax.rsqrt(new_col) * common
+    for k in range(1, n):
+        factor_out[:, column_slice(partner(k))] = lax.rsqrt(messages_in[k - 1, :, :width]) * common
 
 
 def update_kernel(
@@ -192,7 +200,7 @@
             stage[slot, at, :] = (w_ref[at, cols].astype(jnp.float32) - move).astype(jnp.bfloat16)
             return total + lane_sum(move * move)
 
-        total = lax.fori_loop(0, rows // ROWS, body, total)
+        total = lax.fori_loop(0, rows // ROWS, body, total, unroll=UNROLL)
         out_copy(b).start()
         return total
 

time: 37.5 us -> 33.1 us (0.88)
  Pallas kernels: 35.4 us -> 31 us
    pallas_call x1, Pallas kernels: 21.8 us -> 18.9 us  [shards(): pl.pallas_call(functools.partial(statistics_kernel, n, experts), out_shap...]
    pallas_call x1, Pallas kernels: 13.6 us -> 12 us  [shards(): pl.pallas_call(functools.partial(update_kernel, block), out_shape=[jax.Sh...]
where the time goes in v3:
time: 33.1 us; the launch traced here: 32.9 us
  Pallas kernels  31 us (94%)
  between operations  1.93 us (6%)
    pallas_call x1, Pallas kernels, shards(): pl.pallas_call(functools.partial(statistics_kernel, n, experts), out_shap...  18.9 us
    pallas_call x1, Pallas kernels, shards(): pl.pallas_call(functools.partial(update_kernel, block), out_shape=[jax.Sh...  12 us

profile of v3, /device:TPU:0, one launch (start us, length us, event | category | flops | bytes accessed | tf_op | source)
XLA Modules:
  0.0 32.9 jit_solution(4597859387281616469)
XLA Ops:
  1.9 18.9 %statistics.1 = (bf16[512,14336]{1,0:T(8,128)(2,1)S(1)}, bf16[512,14336]{1,0:T(8,128)(2,1)S(1)}, f32[512,128]{1,0:T(8,128)S(1)}, f32[1,14336]{1,0:T(1,128)S(1)},...) custom-call(s32[1]{0:T(128)} %bitcast.5.step_ref, f32[1]{0:T(128)} %bitcast.6.prev_ref, f32[1,512]{1,0:T(1,128)} %row_hbm.1, ...), custom_call_target="tpu_custom_call" | custom-call | tf_op jit(solution)/shard_map/statistics/pallas_call | solution.py:231
  20.9 12.0 %update.1 = (bf16[512,14336]{1,0:T(8,128)(2,1)}, f32[1,512]{1,0:T(1,128)}, f32[1,1792]{1,0:T(1,128)}, f32[1,1]{1,0:T(1,128)}) custom-call(bf16[512,14336]{1,0:T(8,128)(2,1)S(1)} %get-tuple-element.14.g_ref, bf16[512,14336]{1,0:T(8,128)(2,1)S(1)} %get-tuple-element.15.w_ref, f32[512,128]{1,0:T(8,128)S(1)} %get-tuple-element.16.scale_ref, ...), custom_call_target="tpu_custom_call" | custom-call | tf_op jit(solution)/shard_map/update/pallas_call | solution.py:268
